TPU v7x, 128 devices: a whole 4x4x4 slice. The times are simulated.
128 devices in a mesh: band: 8 (over y, x_lo), chan: 16 (over x_hi, z, core).
Axes of the slice: x: 4 (x_hi: 2, x_lo: 2; x = x_hi * 2 + x_lo), y: 4, z: 4, core: 2. Of those that a mesh axis runs over, the one named last changes fastest.
Arguments:
- coeffs: bfloat16 [2, 8, 1024, 8192], P(None, None, 'chan', 'band'), may hold values from -1100 to 1100, as said below
Outputs:
- coherence: float32 [1024, 1024], P('chan', 'band')
Inputs may be any that keep to these rules, and one draw needn't show every extreme that they name: `coeffs`: finite real and imaginary parts.
All inputs are finite; a program needn't handle non-finite values.
Results may differ from a plain program's by a relative error of at most 0.0003.
Values may be sent and summed in bfloat16 or wider, within the bound.
No kernel may reach another device: no remote copies, remote signals or barrier semaphores. Data moves between devices by JAX's collectives and lax.ppermute only.
A program may use at most 192 MiB of HBM per device.

v0:
```python
import jax
import jax.numpy as jnp
from jax import lax
from jax.experimental import pallas as pl
from jax.experimental.pallas import tpu as pltpu
from jax.sharding import Mesh, PartitionSpec as P


K = 8
W = 16
EPS = 1e-06
BANDS = 8

STEPS = ((0, 0), (0, 1), (0, 3), (1, 0), (0, 2), (1, 1), (1, 3), (1, 2))
ORDER = (1, 2, 3, 5, 4, 6, 7)
SPLIT = 3

LIMIT = 2.0**-11
SQUARE = 2.0**8
LINEAR = 2.0**26

WHOLE = pl.BlockSpec(memory_space=pltpu.VMEM)
SCALAR = pl.BlockSpec(memory_space=pltpu.SMEM)
PIECE = (K, BANDS * W, 128)


def chip_at(chip, step, sign):
    half = (chip >> 2) ^ step[0]
    return (half << 2) + ((chip + sign * step[1]) & 3)


def swapped(x):
    return jnp.concatenate((x[:, 64:], x[:, :64]), axis=1)


def call(kernel, mib, out, scratch=(), products=0, aliases=None):
    many = isinstance(out, list)

    def run(place, *args, first=WHOLE):
        return pl.pallas_call(
            kernel,
            in_specs=[SCALAR, first] + [WHOLE] * (len(args) - 1),
            out_specs=[WHOLE] * len(out) if many else WHOLE,
            out_shape=out,
            scratch_shapes=list(scratch),
            input_output_aliases=aliases or {},
            cost_estimate=pl.CostEstimate(
                flops=products * BANDS * 2 * 256**3, bytes_accessed=2**20, transcendentals=0
            ),
            compiler_params=pltpu.CompilerParams(vmem_limit_bytes=mib * 2**20),
        )(place, *args)

    return run


def turn_kernel(steps, place, x_hbm, *refs):
    outs = refs[: len(steps)]
    x_ref, sems = refs[len(steps) :]
    core = place[0]
    chip = place[1]

    def fetch(p, k):
        lanes = pl.ds(pl.multiple_of(chip_at(chip, steps[p], 1) * 128, 128), 128)
        return pltpu.make_async_copy(x_hbm.at[:, k, :, lanes], x_ref.at[p, :, k], sems.at[p, k])

    for k in range(K):
        for p in range(len(steps)):
            fetch(p, k).start()

    def step(h, carry):
        for k in range(K // 2):
            for p in range(len(steps)):
                fetch(p, h * (K // 2) + k).wait()
        for k in range(K // 2):
            for p, o_ref in enumerate(outs):
                first = x_ref[p, core, h * (K // 2) + k]
                second = x_ref[p, 1 - core, h * (K // 2) + k]
                o_ref[h * (K // 2) + k] = jnp.concatenate((first, second), axis=0).T
        return carry

    lax.fori_loop(0, 2, step, 0)


def turned(place, coeffs, steps):
    run = call(
        lambda *refs: turn_kernel(steps, *refs),
        8,
        [jax.ShapeDtypeStruct(PIECE, jnp.bfloat16)] * len(steps),
        (
            pltpu.VMEM((len(steps), 2, K, coeffs.shape[2], 128), jnp.bfloat16),
            pltpu.SemaphoreType.DMA((len(steps), K)),
        ),
    )
    return run(place, coeffs, first=pl.BlockSpec(memory_space=pltpu.HBM))


def arrange_kernel(place, *refs):
    *pieces, right = refs
    side = place[0]
    low = lax.broadcasted_iota(jnp.int32, (128, 128), 1) < 64
    row = lax.broadcasted_iota(jnp.int32, (W, 128), 0)
    for m, (a_ref, b_ref) in enumerate(zip(pieces[::2], pieces[1::2])):

        def step(k, power):
            power = list(power)
            a = a_ref[k]
            b = b_ref[k]
            for part, block in (
                (side, jnp.where(low, a, swapped(b))),
                (1 - side, jnp.where(low, swapped(a), b)),
            ):
                for n in range(BANDS):
                    rows = block[n * W : (n + 1) * W]
                    right[n, m, part * K + k] = rows
                    wide = rows.astype(jnp.float32)
                    wide = wide * wide
                    power[n] += wide[:8] + wide[8:]
            return tuple(power)

        power = (jnp.zeros((8, 128), jnp.float32),) * BANDS
        for k in range(K):
            power = step(k, power)
        for n in range(BANDS):
            inv = 1.0 / (jnp.sum(power[n], axis=0, keepdims=True) + EPS)
            high = inv.astype(jnp.bfloat16).astype(jnp.float32)
            middle = (inv - high).astype(jnp.bfloat16).astype(jnp.float32)
            rest = inv - high - middle
            parts = jnp.where(row == 0, high, jnp.where(row == 1, middle, jnp.where(row == 2, rest, 0.0)))
            right[n, m, 2 * K] = parts.astype(jnp.bfloat16)


def arranged(place, *pieces):
    shape = (BANDS, len(pieces) // 2, 2 * K + 1, W, 128)
    return call(arrange_kernel, 8, jax.ShapeDtypeStruct(shape, jnp.bfloat16), products=1)(place, *pieces)


def inverse(right, n, m):
    parts = right[n, m, 2 * K].astype(jnp.float32)
    return jnp.sum(parts, axis=0, keepdims=True)


def columns(right, n, m):
    return right[n, m, 0 : 2 * K].reshape(256, 128)


def tile_rows(i):
    return pl.ds(i * 128 if isinstance(i, int) else pl.multiple_of(i * 128, 128), 128)


def turn_left(i, right, m, left, col_inv):
    rows = tile_rows(i)
    inv = jnp.concatenate([inverse(right, n, m) for n in range(BANDS)], axis=0).T
    for n in range(BANDS):
        block = columns(right, n, m).T
        left[0, n, rows, :] = block[:, :128]
        left[1, n, rows, :] = block[:, 128:]
        left[2, n, rows, :] = -block[:, :128]
        col_inv[n, rows, :] = jnp.broadcast_to(inv[:, n : n + 1], (128, 128))


def coherence(i, left, col_inv, cols):
    rows = tile_rows(i)
    total = jnp.zeros((128, 128 * len(cols)), jnp.float32)
    for n in range(BANDS):
        re = left[0, n, rows, :]
        im = left[1, n, rows, :]
        for_re = jnp.concatenate((re, im), axis=1)
        for_im = jnp.concatenate((im, left[2, n, rows, :]), axis=1)
        lhs = jnp.concatenate((for_re, for_im), axis=0)
        rhs = jnp.concatenate([columns(right, n, m) for right, m in cols], axis=1)
        both = jnp.dot(lhs, rhs, preferred_element_type=jnp.float32)
        re = both[:128]
        im = both[128:]
        ri = jnp.concatenate([inverse(right, n, m) for right, m in cols], axis=1)
        ci = jnp.concatenate([col_inv[n, rows, :]] * len(cols), axis=1)
        total += (re * re + im * im) * ri * ci
    return total


def no_diagonal(first, total):
    row = lax.broadcasted_iota(jnp.int32, total.shape, 0) + first
    col = lax.broadcasted_iota(jnp.int32, total.shape, 1)
    return jnp.where(row == col, 0.0, total)


def put(place, o_ref, i, b, own, other):
    first_core = place[0] == 0
    chip = place[1]
    low = lax.broadcasted_iota(jnp.int32, (128, 128), 1) < 64
    froms = []
    for h in range(2):
        at = chip_at(chip, STEPS[h], -1)
        for t in range(1, 4):
            at = jnp.where(i == t, chip_at(chip, STEPS[2 * t + h], -1), at)
        froms.append(at)
    for m in range(2):
        lanes = slice(m * 128, (m + 1) * 128)
        zero = jnp.where(first_core, own[:, lanes], other[:, lanes])
        one = jnp.where(first_core, other[:, lanes], own[:, lanes])
        for g in range(2):
            if g == 0:
                sums = jnp.where(low, zero, swapped(one))
            else:
                sums = jnp.where(low, swapped(zero), one)
            coded = jnp.where(sums >= LIMIT, sums * sums * SQUARE, sums * -LINEAR)
            to = chip_at(chip, STEPS[4 * b + 2 * m + g], -1)
            for h in range(2):
                o_ref[froms[h], to] = coded[h * 64 : (h + 1) * 64]


def both_of(right):
    return ((right, 0), (right, 1))


LEFT = jax.ShapeDtypeStruct((3, BANDS, 512, 128), jnp.bfloat16)
COL_INV = jax.ShapeDtypeStruct((BANDS, 512, 128), jnp.float32)
CODED = jax.ShapeDtypeStruct((8, 8, 64, 128), jnp.float32)


def sums(*shape):
    return jax.ShapeDtypeStruct(shape, jnp.float32)


def near_own_kernel(place, right, left, col_inv, o_ref):
    def tile(i, carry):
        turn_left(i, right, i, left, col_inv)
        o_ref[tile_rows(i), :] = no_diagonal(i * 128, coherence(i, left, col_inv, both_of(right)))
        return carry

    lax.fori_loop(0, 2, tile, 0)


def near_other_kernel(place, right, left, col_inv, o_ref):
    def tile(i, carry):
        o_ref[tile_rows(i), :] = coherence(i, left, col_inv, both_of(right))
        return carry

    lax.fori_loop(0, 2, tile, 0)


def next_kernel(
    place, own0, other0, right2, near_sums, near_others, unused0, unused1, left, col_inv, o20, o22, o_ref
):
    turn_left(2, right2, 0, left, col_inv)

    def tile(i, carry):
        rows = tile_rows(i)
        put(place, o_ref, i, 0, near_sums[rows, :], near_others[rows, :])
        return carry

    lax.fori_loop(0, 2, tile, 0)
    own = coherence(2, left, col_inv, both_of(own0))
    o20[...] = own
    put(place, o_ref, 2, 0, own, coherence(2, left, col_inv, both_of(other0)))
    o22[...] = no_diagonal(0, coherence(2, left, col_inv, ((right2, 0),)))


def far_own_kernel(
    place, own0, other0, right2, right3, o20, o22, unused0, unused1, unused2, left, col_inv, own_far, o_ref
):
    turn_left(3, right3, 0, left, col_inv)
    own = coherence(3, left, col_inv, both_of(own0))
    put(place, o_ref, 3, 0, own, coherence(3, left, col_inv, both_of(other0)))
    last = no_diagonal(128, coherence(3, left, col_inv, ((right2, 0), (right3, 0))))
    own_far[384:512, :] = last
    own_far[256:384, 0:128] = o22[...]
    own_far[256:384, 128:256] = last[:, :128].T
    for i in range(2):
        lanes = slice(i * 128, (i + 1) * 128)
        own_far[lanes, 0:128] = o20[:, lanes].T
        own_far[lanes, 128:256] = own[:, lanes].T


def far_other_kernel(place, right2, right3, left, col_inv, own_far, unused, o_ref):
    def tile(i, carry):
        other = coherence(i, left, col_inv, ((right2, 0), (right3, 0)))
        put(place, o_ref, i, 1, own_far[tile_rows(i), :], other)
        return carry

    lax.fori_loop(0, 4, tile, 0)


near_own = call(near_own_kernel, 8, [LEFT, COL_INV, sums(256, 256)], products=2)
near_other = call(near_other_kernel, 8, sums(256, 256), products=2)
next_pairs = call(
    next_kernel,
    8,
    [LEFT, COL_INV, sums(128, 256), sums(128, 128), CODED],
    products=3,
    aliases={6: 0, 7: 1},
)
far_own = call(
    far_own_kernel,
    8,
    [LEFT, COL_INV, sums(512, 256), CODED],
    products=3,
    aliases={7: 0, 8: 1, 9: 3},
)
far_other = call(far_other_kernel, 8, CODED, products=4, aliases={6: 0})


def body(scale, coeffs):
    core = lax.axis_index("core")
    chip = lax.axis_index("chip")
    place = jnp.stack((core, chip)).astype(jnp.int32)
    coeffs = pltpu.with_memory_space_constraint(coeffs, pltpu.HBM)
    pieces = [None] * len(STEPS)
    for some in (ORDER[:SPLIT], ORDER[SPLIT:] + (0,)):
        for p, piece in zip(some, turned(place, coeffs, [STEPS[p] for p in some])):
            pieces[p] = piece
    for p in range(1, len(STEPS)):
        pairs = [(c, chip_at(c, STEPS[p], 1)) for c in range(8)]
        pieces[p] = lax.ppermute(pieces[p], "chip", pairs)
    swap = [(0, 1), (1, 0)]
    own0 = arranged(place, *pieces[:4])
    other0 = lax.ppermute(own0, "core", swap)
    left, col_inv, a00 = near_own(place, own0)
    b00 = near_other(place, other0, left, col_inv)
    own2 = arranged(place, *pieces[4:6])
    other2 = lax.ppermute(own2, "core", swap)
    left, col_inv, o20, o22, coded = next_pairs(place, own0, other0, own2, a00, b00, left, col_inv)
    own3 = arranged(place, *pieces[6:])
    other3 = lax.ppermute(own3, "core", swap)
    left, col_inv, own_far, coded = far_own(
        place, own0, other0, own2, own3, o20, o22, left, col_inv, coded
    )
    coded = far_other(place, other2, other3, left, col_inv, own_far, coded)
    coded = coded.reshape(64, 64, 128).astype(jnp.float16)
    coded = lax.all_to_all(coded, ("chip", "band"), 0, 0, tiled=True).astype(jnp.float32)
    square = coded * lax.rsqrt(coded) * (scale / SQUARE**0.5)
    return jnp.sum(jnp.where(coded > 0, square, coded * (-scale / LINEAR)), axis=0)


def solution(mesh):
    fine = Mesh(mesh.devices.reshape(8, 8, 2), ("band", "chip", "core"))
    scale = W * K / 512

    def step(coeffs):
        return body(scale, coeffs)

    return jax.shard_map(
        step,
        mesh=fine,
        in_specs=(P(None, None, ("chip", "core"), "band"),),
        out_specs=P(("chip", "core"), "band"),
        check_vma=False,
    )
```

profile of v0, /device:TPU:0, one launch (start us, length us, event | category | flops | bytes accessed | tf_op | source)
XLA Modules:
  0.0 81.7 jit_solution(3445946452755951602)
XLA Ops:
  0.1 2.0 %shard_map.20 = (bf16[8,128,128]{2,1,0:T(8,128)(2,1)S(1)}, bf16[8,128,128]{2,1,0:T(8,128)(2,1)S(1)}, bf16[8,128,128]{2,1,0:T(8,128)(2,1)S(1)}) custom-call(s32[2]{0:T(128)S(1)} %pad_add_fusion.refs_0_.place, bf16[2,8,64,1024]{3,2,1,0:T(8,128)(2,1)} %refs_1_.3), custom_call_target="tpu_custom_call" | custom-call | bytes 1048576 | tf_op jit(solution)/shard_map/pallas_call | solution.py:40
  2.1 2.1 %collective-permute-start.6 = (bf16[8,128,128]{2,1,0:T(8,128)(2,1)S(1)}, bf16[8,128,128]{2,1,0:T(8,128)(2,1)S(1)}, u32[]{:S(2)}, u32[]{:S(2)}) collective-permute-start(bf16[8,128,128]{2,1,0:T(8,128)(2,1)S(1)} %get-tuple-element.30), channel_id=1, source_target_pairs={{0,2},{2,4},{4,6},{6,0},{8,10},{10,12},{12,14},{14,8},{1,3},{3,5},... | collective-permute-start | bytes 786440 | tf_op jit(solution)/shard_map/ppermute | solution.py:313
  4.2 2.2 %collective-permute-start.7 = (bf16[8,128,128]{2,1,0:T(8,128)(2,1)S(1)}, bf16[8,128,128]{2,1,0:T(8,128)(2,1)S(1)}, u32[]{:S(2)}, u32[]{:S(2)}) collective-permute-start(bf16[8,128,128]{2,1,0:T(8,128)(2,1)S(1)} %get-tuple-element.31), channel_id=1, source_target_pairs={{0,6},{2,0},{4,2},{6,4},{8,14},{10,8},{12,10},{14,12},{1,7},{3,1},... | collective-permute-start | bytes 786440 | tf_op jit(solution)/shard_map/ppermute | solution.py:313
  6.4 3.0 %collective-permute-start.8 = (bf16[8,128,128]{2,1,0:T(8,128)(2,1)S(1)}, bf16[8,128,128]{2,1,0:T(8,128)(2,1)S(1)}, u32[]{:S(2)}, u32[]{:S(2)}) collective-permute-start(bf16[8,128,128]{2,1,0:T(8,128)(2,1)S(1)} %get-tuple-element.32), channel_id=1, source_target_pairs={{0,8},{2,10},{4,12},{6,14},{8,0},{10,2},{12,4},{14,6},{1,9},{3,11}... | collective-permute-start | bytes 786440 | tf_op jit(solution)/shard_map/ppermute | solution.py:313
  9.4 2.5 %shard_map.17 = (bf16[8,128,128]{2,1,0:T(8,128)(2,1)S(1)}, bf16[8,128,128]{2,1,0:T(8,128)(2,1)S(1)}, bf16[8,128,128]{2,1,0:T(8,128)(2,1)S(1)}, bf16[8,128,128]{2,1,0:T(8,128)(2,1)S(1)}, bf16[8,128,128]{2,1,0:T(8,128)(2,1)S(1)}) custom-call(s32[2]{0:T(128)S(1)} %pad_add_fusion.refs_0_.place, bf16[2,8,64,1024]{3,2,1,0:T(8,128)(2,1)} %refs_1_.3), custom_call_target="tpu_custom_call" | custom-call | bytes 1048576 | tf_op jit(solution)/shard_map/pallas_call | solution.py:40
  11.9 0.7 collective-permute-done.6.refs_1_
  12.7 3.0 %collective-permute-done.8.refs_3_ = bf16[8,128,128]{2,1,0:T(8,128)(2,1)S(1)} collective-permute-done((bf16[8,128,128]{2,1,0:T(8,128)(2,1)S(1)}, bf16[8,128,128]{2,1,0:T(8,128)(2,1)S(1)}, u32[]{:S(2)}, u32[]{:S(2)}) %collective-permute-start.8) | collective-permute-done | bytes 262176 | tf_op jit(solution)/shard_map/ppermute | solution.py:313
  15.7 1.0 %shard_map.21.right.own0 = bf16[8,2,17,16,128]{4,3,2,1,0:T(8,128)(2,1)S(1)} custom-call(s32[2]{0:T(128)S(1)} %pad_add_fusion.refs_0_.place, bf16[8,128,128]{2,1,0:T(8,128)(2,1)S(1)} %get-tuple-element.29.refs_0_, bf16[8,128,128]{2,1,0:T(8,128)(2,1)S(1)} %collective-permute-done.6.refs_1_, bf16[8,128,128]{2,1,0:T(8,128)(2,1)S(1)} %collective-permute-done.7.refs_2_, ...), custom_call_target="tpu_custom_call" | custom-call | flops 268435456 | bytes 1048576 | tf_op jit(solution)/shard_map/pallas_call | solution.py:40
  16.8 1.6 %collective-permute-start = (bf16[8,128,128]{2,1,0:T(8,128)(2,1)S(1)}, bf16[8,128,128]{2,1,0:T(8,128)(2,1)S(1)}, u32[]{:S(2)}, u32[]{:S(2)}) collective-permute-start(bf16[8,128,128]{2,1,0:T(8,128)(2,1)S(1)} %get-tuple-element.25), channel_id=1, source_target_pairs={{0,4},{2,6},{4,0},{6,2},{8,12},{10,14},{12,8},{14,10},{1,5},{3,7},... | collective-permute-start | bytes 786440 | tf_op jit(solution)/shard_map/ppermute | solution.py:313
  18.4 3.5 %collective-permute-start.1 = (bf16[8,128,128]{2,1,0:T(8,128)(2,1)S(1)}, bf16[8,128,128]{2,1,0:T(8,128)(2,1)S(1)}, u32[]{:S(2)}, u32[]{:S(2)}) collective-permute-start(bf16[8,128,128]{2,1,0:T(8,128)(2,1)S(1)} %get-tuple-element.26), channel_id=1, source_target_pairs={{0,10},{2,12},{4,14},{6,8},{8,2},{10,4},{12,6},{14,0},{1,11},{3,13... | collective-permute-start | bytes 786440 | tf_op jit(solution)/shard_map/ppermute | solution.py:313
  21.9 2.2 %collective-permute-start.3 = (bf16[8,128,128]{2,1,0:T(8,128)(2,1)S(1)}, bf16[8,128,128]{2,1,0:T(8,128)(2,1)S(1)}, u32[]{:S(2)}, u32[]{:S(2)}) collective-permute-start(bf16[8,128,128]{2,1,0:T(8,128)(2,1)S(1)} %get-tuple-element.27), channel_id=1, source_target_pairs={{0,14},{2,8},{4,10},{6,12},{8,6},{10,0},{12,2},{14,4},{1,15},{3,9}... | collective-permute-start | bytes 786440 | tf_op jit(solution)/shard_map/ppermute | solution.py:313
  24.0 3.3 %collective-permute-start.4 = (bf16[8,128,128]{2,1,0:T(8,128)(2,1)S(1)}, bf16[8,128,128]{2,1,0:T(8,128)(2,1)S(1)}, u32[]{:S(2)}, u32[]{:S(2)}) collective-permute-start(bf16[8,128,128]{2,1,0:T(8,128)(2,1)S(1)} %get-tuple-element.28), channel_id=1, source_target_pairs={{0,12},{2,14},{4,8},{6,10},{8,4},{10,6},{12,0},{14,2},{1,13},{3,15... | collective-permute-start | bytes 786440 | tf_op jit(solution)/shard_map/ppermute | solution.py:313
  27.3 6.1 %collective-permute-done.refs_0_ = bf16[8,128,128]{2,1,0:T(8,128)(2,1)S(1)} collective-permute-done((bf16[8,128,128]{2,1,0:T(8,128)(2,1)S(1)}, bf16[8,128,128]{2,1,0:T(8,128)(2,1)S(1)}, u32[]{:S(2)}, u32[]{:S(2)}) %collective-permute-start) | collective-permute-done | bytes 262176 | tf_op jit(solution)/shard_map/ppermute | solution.py:313
  33.4 0.8 shard_map.18.right2
  34.3 1.8 %collective-permute-done.3.refs_0_ = bf16[8,128,128]{2,1,0:T(8,128)(2,1)S(1)} collective-permute-done((bf16[8,128,128]{2,1,0:T(8,128)(2,1)S(1)}, bf16[8,128,128]{2,1,0:T(8,128)(2,1)S(1)}, u32[]{:S(2)}, u32[]{:S(2)}) %collective-permute-start.3) | collective-permute-done | bytes 262176 | tf_op jit(solution)/shard_map/ppermute | solution.py:313
  36.1 4.7 %collective-permute-done.4.refs_1_ = bf16[8,128,128]{2,1,0:T(8,128)(2,1)S(1)} collective-permute-done((bf16[8,128,128]{2,1,0:T(8,128)(2,1)S(1)}, bf16[8,128,128]{2,1,0:T(8,128)(2,1)S(1)}, u32[]{:S(2)}, u32[]{:S(2)}) %collective-permute-start.4) | collective-permute-done | bytes 262176 | tf_op jit(solution)/shard_map/ppermute | solution.py:313
  40.7 0.8 shard_map.19.right3
  41.6 1.7 %shard_map.22 = (bf16[3,8,512,128]{3,2,1,0:T(8,128)(2,1)S(1)}, f32[8,512,128]{2,1,0:T(8,128)S(1)}, f32[256,256]{1,0:T(8,128)S(1)}) custom-call(s32[2]{0:T(128)S(1)} %pad_add_fusion.refs_0_.place, bf16[8,2,17,16,128]{4,3,2,1,0:T(8,128)(2,1)S(1)} %shard_map.21.right.own0), custom_call_target="tpu_custom_call" | custom-call | flops 536870912 | bytes 1048576 | tf_op jit(solution)/shard_map/pallas_call | solution.py:40
  43.4 1.5 %shard_map.23.near_others = f32[256,256]{1,0:T(8,128)S(1)} custom-call(s32[2]{0:T(128)S(1)} %pad_add_fusion.refs_0_.place, bf16[8,2,17,16,128]{4,3,2,1,0:T(8,128)(2,1)S(1)} %collective-permute-done.9.right.other0, bf16[3,8,512,128]{3,2,1,0:T(8,128)(2,1)S(1)} %get-tuple-element.34.left.unused0, f32[8,512,128]{2,1,0:T(8,128)S(1)} %get-tuple-element.35.col_inv.unused1), custom_call_target="tpu_custom_call" | custom-call | flops 536870912 | bytes 1048576 | tf_op jit(solution)/shard_map/pallas_call | solution.py:40
  44.9 2.4 %shard_map.24 = (bf16[3,8,512,128]{3,2,1,0:T(8,128)(2,1)S(1)}, f32[8,512,128]{2,1,0:T(8,128)S(1)}, f32[128,256]{1,0:T(8,128)S(1)}, f32[128,128]{1,0:T(8,128)S(1)}, f32[8,8,64,128]{3,2,1,0:T(8,128)S(1)}) custom-call(s32[2]{0:T(128)S(1)} %pad_add_fusion.refs_0_.place, ...), custom_call_target="tpu_custom_call", output_to_operand_aliasing={{0}: (6, {}), {1}: (7, {})} | custom-call | flops 805306368 | bytes 1048576 | tf_op jit(solution)/shard_map/pallas_call | solution.py:40
  47.2 2.0 %shard_map.25 = (bf16[3,8,512,128]{3,2,1,0:T(8,128)(2,1)S(1)}, f32[8,512,128]{2,1,0:T(8,128)S(1)}, f32[512,256]{1,0:T(8,128)S(1)}, f32[8,8,64,128]{3,2,1,0:T(8,128)S(1)}) custom-call(s32[2]{0:T(128)S(1)} %pad_add_fusion.refs_0_.place, ...), custom_call_target="tpu_custom_call", output_to_operand_aliasing={{0}: (7, {}), {1}: (8, {}), {3}: (9, {})} | custom-call | flops 805306368 | bytes 1048576 | tf_op jit(solution)/shard_map/pallas_call | solution.py:40
  49.3 2.9 %shard_map.26 = f32[8,8,64,128]{3,2,1,0:T(8,128)S(1)} custom-call(s32[2]{0:T(128)S(1)} %pad_add_fusion.refs_0_.place, bf16[8,1,17,16,128]{4,3,2,1,0:T(8,128)(2,1)S(1)} %collective-permute-done.2.right2, bf16[8,1,17,16,128]{4,3,2,1,0:T(8,128)(2,1)S(1)} %collective-permute-done.5.right3, ...), custom_call_target="tpu_custom_call", output_to_operand_aliasing={{}: (6, {})} | custom-call | flops 1073741824 | bytes 1048576 | tf_op jit(solution)/shard_map/pallas_call | solution.py:40
  52.4 28.1 %all_to_all.5 = f16[64,64,128]{2,1,0:T(8,128)(2,1)S(1)} all-to-all(f16[64,64,128]{2,1,0:T(8,128)(2,1)S(1)} %bitcast.3), channel_id=1, replica_groups=mesh['band'=8,'chip'=8,'core'=2] {'chip','band'}, dimensions={0} | all-to-all | bytes 2097152 | tf_op jit(solution)/shard_map/all_to_all | solution.py:329
  80.5 1.2 %fusion.2 = f32[64,128]{1,0:T(8,128)} fusion(f16[64,64,128]{2,1,0:T(8,128)(2,1)S(1)} %all_to_all.5), kind=kLoop, calls=%fused_computation.6 | loop fusion | flops 3661824 | bytes 1081344 | tf_op jit(solution)/shard_map/reduce_sum | solution.py:331
  (10 shorter events, 0.6 us)
Async XLA Ops:
  2.1 10.5 %collective-permute-start.6 = (bf16[8,128,128]{2,1,0:T(8,128)(2,1)S(1)}, bf16[8,128,128]{2,1,0:T(8,128)(2,1)S(1)}, u32[]{:S(2)}, u32[]{:S(2)}) collective-permute-start(bf16[8,128,128]{2,1,0:T(8,128)(2,1)S(1)} %get-tuple-element.30), channel_id=1, source_target_pairs={{0,2},{2,4},{4,6},{6,0},{8,10},{10,12},{12,14},{14,8},{1,3},{3,5},... | collective-permute-start | bytes 786440 | tf_op jit(solution)/shard_map/ppermute | solution.py:313
  4.2 8.4 %collective-permute-start.7 = (bf16[8,128,128]{2,1,0:T(8,128)(2,1)S(1)}, bf16[8,128,128]{2,1,0:T(8,128)(2,1)S(1)}, u32[]{:S(2)}, u32[]{:S(2)}) collective-permute-start(bf16[8,128,128]{2,1,0:T(8,128)(2,1)S(1)} %get-tuple-element.31), channel_id=1, source_target_pairs={{0,6},{2,0},{4,2},{6,4},{8,14},{10,8},{12,10},{14,12},{1,7},{3,1},... | collective-permute-start | bytes 786440 | tf_op jit(solution)/shard_map/ppermute | solution.py:313
  6.4 9.3 %collective-permute-start.8 = (bf16[8,128,128]{2,1,0:T(8,128)(2,1)S(1)}, bf16[8,128,128]{2,1,0:T(8,128)(2,1)S(1)}, u32[]{:S(2)}, u32[]{:S(2)}) collective-permute-start(bf16[8,128,128]{2,1,0:T(8,128)(2,1)S(1)} %get-tuple-element.32), channel_id=1, source_target_pairs={{0,8},{2,10},{4,12},{6,14},{8,0},{10,2},{12,4},{14,6},{1,9},{3,11}... | collective-permute-start | bytes 786440 | tf_op jit(solution)/shard_map/ppermute | solution.py:313
  16.7 26.7 %collective-permute-start.9 = (bf16[8,2,17,16,128]{4,3,2,1,0:T(8,128)(2,1)S(1)}, bf16[8,2,17,16,128]{4,3,2,1,0:T(8,128)(2,1)S(1)}, u32[]{:S(2)}, u32[]{:S(2)}) collective-permute-start(bf16[8,2,17,16,128]{4,3,2,1,0:T(8,128)(2,1)S(1)} %shard_map.21.right.own0), channel_id=1, source_target_pairs={{0,1},{1,0},{2,3},{3,2},{4,5},{5,4},{6,7},{7,6},{8,9},{9,8},{10,11... | collective-permute-start | bytes 3342344 | tf_op jit(solution)/shard_map/ppermute | solution.py:316
  16.8 16.6 %collective-permute-start = (bf16[8,128,128]{2,1,0:T(8,128)(2,1)S(1)}, bf16[8,128,128]{2,1,0:T(8,128)(2,1)S(1)}, u32[]{:S(2)}, u32[]{:S(2)}) collective-permute-start(bf16[8,128,128]{2,1,0:T(8,128)(2,1)S(1)} %get-tuple-element.25), channel_id=1, source_target_pairs={{0,4},{2,6},{4,0},{6,2},{8,12},{10,14},{12,8},{14,10},{1,5},{3,7},... | collective-permute-start | bytes 786440 | tf_op jit(solution)/shard_map/ppermute | solution.py:313
  18.4 15.0 %collective-permute-start.1 = (bf16[8,128,128]{2,1,0:T(8,128)(2,1)S(1)}, bf16[8,128,128]{2,1,0:T(8,128)(2,1)S(1)}, u32[]{:S(2)}, u32[]{:S(2)}) collective-permute-start(bf16[8,128,128]{2,1,0:T(8,128)(2,1)S(1)} %get-tuple-element.26), channel_id=1, source_target_pairs={{0,10},{2,12},{4,14},{6,8},{8,2},{10,4},{12,6},{14,0},{1,11},{3,13... | collective-permute-start | bytes 786440 | tf_op jit(solution)/shard_map/ppermute | solution.py:313
  21.9 14.2 %collective-permute-start.3 = (bf16[8,128,128]{2,1,0:T(8,128)(2,1)S(1)}, bf16[8,128,128]{2,1,0:T(8,128)(2,1)S(1)}, u32[]{:S(2)}, u32[]{:S(2)}) collective-permute-start(bf16[8,128,128]{2,1,0:T(8,128)(2,1)S(1)} %get-tuple-element.27), channel_id=1, source_target_pairs={{0,14},{2,8},{4,10},{6,12},{8,6},{10,0},{12,2},{14,4},{1,15},{3,9}... | collective-permute-start | bytes 786440 | tf_op jit(solution)/shard_map/ppermute | solution.py:313
  24.0 16.7 %collective-permute-start.4 = (bf16[8,128,128]{2,1,0:T(8,128)(2,1)S(1)}, bf16[8,128,128]{2,1,0:T(8,128)(2,1)S(1)}, u32[]{:S(2)}, u32[]{:S(2)}) collective-permute-start(bf16[8,128,128]{2,1,0:T(8,128)(2,1)S(1)} %get-tuple-element.28), channel_id=1, source_target_pairs={{0,12},{2,14},{4,8},{6,10},{8,4},{10,6},{12,0},{14,2},{1,13},{3,15... | collective-permute-start | bytes 786440 | tf_op jit(solution)/shard_map/ppermute | solution.py:313
  34.2 15.0 %collective-permute-start.2 = (bf16[8,1,17,16,128]{4,3,2,1,0:T(8,128)(2,1)S(1)}, bf16[8,1,17,16,128]{4,3,2,1,0:T(8,128)(2,1)S(1)}, u32[]{:S(2)}, u32[]{:S(2)}) collective-permute-start(bf16[8,1,17,16,128]{4,3,2,1,0:T(8,128)(2,1)S(1)} %shard_map.18.right2), channel_id=1, source_target_pairs={{0,1},{1,0},{2,3},{3,2},{4,5},{5,4},{6,7},{7,6},{8,9},{9,8},{10,11... | collective-permute-start | bytes 1671176 | tf_op jit(solution)/shard_map/ppermute | solution.py:320
  41.6 7.7 %collective-permute-start.5 = (bf16[8,1,17,16,128]{4,3,2,1,0:T(8,128)(2,1)S(1)}, bf16[8,1,17,16,128]{4,3,2,1,0:T(8,128)(2,1)S(1)}, u32[]{:S(2)}, u32[]{:S(2)}) collective-permute-start(bf16[8,1,17,16,128]{4,3,2,1,0:T(8,128)(2,1)S(1)} %shard_map.19.right3), channel_id=1, source_target_pairs={{0,1},{1,0},{2,3},{3,2},{4,5},{5,4},{6,7},{7,6},{8,9},{9,8},{10,11... | collective-permute-start | bytes 1671176 | tf_op jit(solution)/shard_map/ppermute | solution.py:323
where the time goes:
time: 82.1 us; the launch traced here: 81.7 us
  blocking collectives  28.1 us (34%)
  starting transfers between devices  18.1 us (22%)
  Pallas kernels  17.5 us (21%)
  waiting for transfers between devices  16.3 us (20%)
  other arithmetic  1.48 us (2%)
    all_to_all x1, blocking collectives, body(): lax.all_to_all(coded, ('chip', 'band'), 0, 0, tiled=True)  28.1 us
    ppermute x7, starting transfers between devices, body(): pieces[p] = lax.ppermute(pieces[p], 'chip', pairs)  17.8 us
    pallas_call x10, Pallas kernels, run(): pl.pallas_call(kernel, in_specs=[SCALAR, first] + [WHOLE] * (len(args) -...  17.5 us
    ppermute x7, waiting for transfers between devices, body(): pieces[p] = lax.ppermute(pieces[p], 'chip', pairs)  16.3 us
  transfers between devices with their start and end apart: 10, of which 5 were waited for; matrix products, arithmetic and copies ran while one was open for 0% of the time, Pallas kernels for 14%

commit v1 on v0

--- a/solution.py
+++ b/solution.py
@@ -59,18 +59,16 @@
     core = place[0]
     chip = place[1]
 
-    def fetch(p, k):
+    def fetch(p):
         lanes = pl.ds(pl.multiple_of(chip_at(chip, steps[p], 1) * 128, 128), 128)
-        return pltpu.make_async_copy(x_hbm.at[:, k, :, lanes], x_ref.at[p, :, k], sems.at[p, k])
-
-    for k in range(K):
-        for p in range(len(steps)):
-            fetch(p, k).start()
+        return pltpu.make_async_copy(x_hbm.at[:, :, :, lanes], x_ref.at[p], sems.at[p])
+
+    for p in range(len(steps)):
+        fetch(p).start()
+    for p in range(len(steps)):
+        fetch(p).wait()
 
     def step(h, carry):
-        for k in range(K // 2):
-            for p in range(len(steps)):
-                fetch(p, h * (K // 2) + k).wait()
         for k in range(K // 2):
             for p, o_ref in enumerate(outs):
                 first = x_ref[p, core, h * (K // 2) + k]
@@ -88,7 +86,7 @@
         [jax.ShapeDtypeStruct(PIECE, jnp.bfloat16)] * len(steps),
         (
             pltpu.VMEM((len(steps), 2, K, coeffs.shape[2], 128), jnp.bfloat16),
-            pltpu.SemaphoreType.DMA((len(steps), K)),
+            pltpu.SemaphoreType.DMA((len(steps),)),
         ),
     )
     return run(place, coeffs, first=pl.BlockSpec(memory_space=pltpu.HBM))
@@ -327,8 +325,8 @@
     coded = far_other(place, other2, other3, left, col_inv, own_far, coded)
     coded = coded.reshape(64, 64, 128).astype(jnp.float16)
     coded = lax.all_to_all(coded, ("chip", "band"), 0, 0, tiled=True).astype(jnp.float32)
-    square = coded * lax.rsqrt(coded) * (scale / SQUARE**0.5)
-    return jnp.sum(jnp.where(coded > 0, square, coded * (-scale / LINEAR)), axis=0)
+    value = coded * jnp.where(coded > 0, lax.rsqrt(coded), -(SQUARE**0.5) / LINEAR)
+    return jnp.sum(value, axis=0) * (scale / SQUARE**0.5)
 
 
 def solution(mesh):

time: 82.1 us -> 81.8 us (level)
  no operation moved by 1% of the time
where the time goes in v1:
time: 81.8 us; the launch traced here: 81.6 us
  blocking collectives  28.1 us (34%)
  starting transfers between devices  18.1 us (22%)
  Pallas kernels  17.4 us (21%)
  waiting for transfers between devices  16.5 us (20%)
  other arithmetic  1.36 us (2%)
    all_to_all x1, blocking collectives, body(): lax.all_to_all(coded, ('chip', 'band'), 0, 0, tiled=True)  28.1 us
    ppermute x7, starting transfers between devices, body(): pieces[p] = lax.ppermute(pieces[p], 'chip', pairs)  17.8 us
    pallas_call x10, Pallas kernels, run(): pl.pallas_call(kernel, in_specs=[SCALAR, first] + [WHOLE] * (len(args) -...  17.4 us
    ppermute x7, waiting for transfers between devices, body(): pieces[p] = lax.ppermute(pieces[p], 'chip', pairs)  16.4 us
  transfers between devices with their start and end apart: 10, of which 5 were waited for; matrix products, arithmetic and copies ran while one was open for 0% of the time, Pallas kernels for 14%

profile of v1, /device:TPU:0, one launch (start us, length us, event | category | flops | bytes accessed | tf_op | source)
XLA Modules:
  0.0 81.6 jit_solution(6071492261965889534)
XLA Ops:
  0.1 2.0 %shard_map.20 = (bf16[8,128,128]{2,1,0:T(8,128)(2,1)S(1)}, bf16[8,128,128]{2,1,0:T(8,128)(2,1)S(1)}, bf16[8,128,128]{2,1,0:T(8,128)(2,1)S(1)}) custom-call(s32[2]{0:T(128)S(1)} %pad_add_fusion.refs_0_.place, bf16[2,8,64,1024]{3,2,1,0:T(8,128)(2,1)} %refs_1_.3), custom_call_target="tpu_custom_call" | custom-call | bytes 1048576 | tf_op jit(solution)/shard_map/pallas_call | solution.py:40
  2.1 2.1 %collective-permute-start.6 = (bf16[8,128,128]{2,1,0:T(8,128)(2,1)S(1)}, bf16[8,128,128]{2,1,0:T(8,128)(2,1)S(1)}, u32[]{:S(2)}, u32[]{:S(2)}) collective-permute-start(bf16[8,128,128]{2,1,0:T(8,128)(2,1)S(1)} %get-tuple-element.30), channel_id=1, source_target_pairs={{0,2},{2,4},{4,6},{6,0},{8,10},{10,12},{12,14},{14,8},{1,3},{3,5},... | collective-permute-start | bytes 786440 | tf_op jit(solution)/shard_map/ppermute | solution.py:311
  4.2 2.2 %collective-permute-start.7 = (bf16[8,128,128]{2,1,0:T(8,128)(2,1)S(1)}, bf16[8,128,128]{2,1,0:T(8,128)(2,1)S(1)}, u32[]{:S(2)}, u32[]{:S(2)}) collective-permute-start(bf16[8,128,128]{2,1,0:T(8,128)(2,1)S(1)} %get-tuple-element.31), channel_id=1, source_target_pairs={{0,6},{2,0},{4,2},{6,4},{8,14},{10,8},{12,10},{14,12},{1,7},{3,1},... | collective-permute-start | bytes 786440 | tf_op jit(solution)/shard_map/ppermute | solution.py:311
  6.4 3.0 %collective-permute-start.8 = (bf16[8,128,128]{2,1,0:T(8,128)(2,1)S(1)}, bf16[8,128,128]{2,1,0:T(8,128)(2,1)S(1)}, u32[]{:S(2)}, u32[]{:S(2)}) collective-permute-start(bf16[8,128,128]{2,1,0:T(8,128)(2,1)S(1)} %get-tuple-element.32), channel_id=1, source_target_pairs={{0,8},{2,10},{4,12},{6,14},{8,0},{10,2},{12,4},{14,6},{1,9},{3,11}... | collective-permute-start | bytes 786440 | tf_op jit(solution)/shard_map/ppermute | solution.py:311
  9.4 2.3 %shard_map.17 = (bf16[8,128,128]{2,1,0:T(8,128)(2,1)S(1)}, bf16[8,128,128]{2,1,0:T(8,128)(2,1)S(1)}, bf16[8,128,128]{2,1,0:T(8,128)(2,1)S(1)}, bf16[8,128,128]{2,1,0:T(8,128)(2,1)S(1)}, bf16[8,128,128]{2,1,0:T(8,128)(2,1)S(1)}) custom-call(s32[2]{0:T(128)S(1)} %pad_add_fusion.refs_0_.place, bf16[2,8,64,1024]{3,2,1,0:T(8,128)(2,1)} %refs_1_.3), custom_call_target="tpu_custom_call" | custom-call | bytes 1048576 | tf_op jit(solution)/shard_map/pallas_call | solution.py:40
  11.8 0.9 %collective-permute-done.6.refs_1_ = bf16[8,128,128]{2,1,0:T(8,128)(2,1)S(1)} collective-permute-done((bf16[8,128,128]{2,1,0:T(8,128)(2,1)S(1)}, bf16[8,128,128]{2,1,0:T(8,128)(2,1)S(1)}, u32[]{:S(2)}, u32[]{:S(2)}) %collective-permute-start.6) | collective-permute-done | bytes 262176 | tf_op jit(solution)/shard_map/ppermute | solution.py:311
  12.6 3.0 %collective-permute-done.8.refs_3_ = bf16[8,128,128]{2,1,0:T(8,128)(2,1)S(1)} collective-permute-done((bf16[8,128,128]{2,1,0:T(8,128)(2,1)S(1)}, bf16[8,128,128]{2,1,0:T(8,128)(2,1)S(1)}, u32[]{:S(2)}, u32[]{:S(2)}) %collective-permute-start.8) | collective-permute-done | bytes 262176 | tf_op jit(solution)/shard_map/ppermute | solution.py:311
  15.7 1.0 %shard_map.21.right.own0 = bf16[8,2,17,16,128]{4,3,2,1,0:T(8,128)(2,1)S(1)} custom-call(s32[2]{0:T(128)S(1)} %pad_add_fusion.refs_0_.place, bf16[8,128,128]{2,1,0:T(8,128)(2,1)S(1)} %get-tuple-element.29.refs_0_, bf16[8,128,128]{2,1,0:T(8,128)(2,1)S(1)} %collective-permute-done.6.refs_1_, bf16[8,128,128]{2,1,0:T(8,128)(2,1)S(1)} %collective-permute-done.7.refs_2_, ...), custom_call_target="tpu_custom_call" | custom-call | flops 268435456 | bytes 1048576 | tf_op jit(solution)/shard_map/pallas_call | solution.py:40
  16.8 1.6 %collective-permute-start = (bf16[8,128,128]{2,1,0:T(8,128)(2,1)S(1)}, bf16[8,128,128]{2,1,0:T(8,128)(2,1)S(1)}, u32[]{:S(2)}, u32[]{:S(2)}) collective-permute-start(bf16[8,128,128]{2,1,0:T(8,128)(2,1)S(1)} %get-tuple-element.25), channel_id=1, source_target_pairs={{0,4},{2,6},{4,0},{6,2},{8,12},{10,14},{12,8},{14,10},{1,5},{3,7},... | collective-permute-start | bytes 786440 | tf_op jit(solution)/shard_map/ppermute | solution.py:311
  18.3 3.5 %collective-permute-start.1 = (bf16[8,128,128]{2,1,0:T(8,128)(2,1)S(1)}, bf16[8,128,128]{2,1,0:T(8,128)(2,1)S(1)}, u32[]{:S(2)}, u32[]{:S(2)}) collective-permute-start(bf16[8,128,128]{2,1,0:T(8,128)(2,1)S(1)} %get-tuple-element.26), channel_id=1, source_target_pairs={{0,10},{2,12},{4,14},{6,8},{8,2},{10,4},{12,6},{14,0},{1,11},{3,13... | collective-permute-start | bytes 786440 | tf_op jit(solution)/shard_map/ppermute | solution.py:311
  21.8 2.2 %collective-permute-start.3 = (bf16[8,128,128]{2,1,0:T(8,128)(2,1)S(1)}, bf16[8,128,128]{2,1,0:T(8,128)(2,1)S(1)}, u32[]{:S(2)}, u32[]{:S(2)}) collective-permute-start(bf16[8,128,128]{2,1,0:T(8,128)(2,1)S(1)} %get-tuple-element.27), channel_id=1, source_target_pairs={{0,14},{2,8},{4,10},{6,12},{8,6},{10,0},{12,2},{14,4},{1,15},{3,9}... | collective-permute-start | bytes 786440 | tf_op jit(solution)/shard_map/ppermute | solution.py:311
  24.0 3.3 %collective-permute-start.4 = (bf16[8,128,128]{2,1,0:T(8,128)(2,1)S(1)}, bf16[8,128,128]{2,1,0:T(8,128)(2,1)S(1)}, u32[]{:S(2)}, u32[]{:S(2)}) collective-permute-start(bf16[8,128,128]{2,1,0:T(8,128)(2,1)S(1)} %get-tuple-element.28), channel_id=1, source_target_pairs={{0,12},{2,14},{4,8},{6,10},{8,4},{10,6},{12,0},{14,2},{1,13},{3,15... | collective-permute-start | bytes 786440 | tf_op jit(solution)/shard_map/ppermute | solution.py:311
  27.3 6.1 %collective-permute-done.refs_0_ = bf16[8,128,128]{2,1,0:T(8,128)(2,1)S(1)} collective-permute-done((bf16[8,128,128]{2,1,0:T(8,128)(2,1)S(1)}, bf16[8,128,128]{2,1,0:T(8,128)(2,1)S(1)}, u32[]{:S(2)}, u32[]{:S(2)}) %collective-permute-start) | collective-permute-done | bytes 262176 | tf_op jit(solution)/shard_map/ppermute | solution.py:311
  33.4 0.8 shard_map.18.right2
  34.3 1.8 %collective-permute-done.3.refs_0_ = bf16[8,128,128]{2,1,0:T(8,128)(2,1)S(1)} collective-permute-done((bf16[8,128,128]{2,1,0:T(8,128)(2,1)S(1)}, bf16[8,128,128]{2,1,0:T(8,128)(2,1)S(1)}, u32[]{:S(2)}, u32[]{:S(2)}) %collective-permute-start.3) | collective-permute-done | bytes 262176 | tf_op jit(solution)/shard_map/ppermute | solution.py:311
  36.0 4.7 %collective-permute-done.4.refs_1_ = bf16[8,128,128]{2,1,0:T(8,128)(2,1)S(1)} collective-permute-done((bf16[8,128,128]{2,1,0:T(8,128)(2,1)S(1)}, bf16[8,128,128]{2,1,0:T(8,128)(2,1)S(1)}, u32[]{:S(2)}, u32[]{:S(2)}) %collective-permute-start.4) | collective-permute-done | bytes 262176 | tf_op jit(solution)/shard_map/ppermute | solution.py:311
  40.7 0.8 shard_map.19.right3
  41.6 1.7 %shard_map.22 = (bf16[3,8,512,128]{3,2,1,0:T(8,128)(2,1)S(1)}, f32[8,512,128]{2,1,0:T(8,128)S(1)}, f32[256,256]{1,0:T(8,128)S(1)}) custom-call(s32[2]{0:T(128)S(1)} %pad_add_fusion.refs_0_.place, bf16[8,2,17,16,128]{4,3,2,1,0:T(8,128)(2,1)S(1)} %shard_map.21.right.own0), custom_call_target="tpu_custom_call" | custom-call | flops 536870912 | bytes 1048576 | tf_op jit(solution)/shard_map/pallas_call | solution.py:40
  43.4 1.5 %shard_map.23.near_others = f32[256,256]{1,0:T(8,128)S(1)} custom-call(s32[2]{0:T(128)S(1)} %pad_add_fusion.refs_0_.place, bf16[8,2,17,16,128]{4,3,2,1,0:T(8,128)(2,1)S(1)} %collective-permute-done.9.right.other0, bf16[3,8,512,128]{3,2,1,0:T(8,128)(2,1)S(1)} %get-tuple-element.34.left.unused0, f32[8,512,128]{2,1,0:T(8,128)S(1)} %get-tuple-element.35.col_inv.unused1), custom_call_target="tpu_custom_call" | custom-call | flops 536870912 | bytes 1048576 | tf_op jit(solution)/shard_map/pallas_call | solution.py:40
  44.8 2.4 %shard_map.24 = (bf16[3,8,512,128]{3,2,1,0:T(8,128)(2,1)S(1)}, f32[8,512,128]{2,1,0:T(8,128)S(1)}, f32[128,256]{1,0:T(8,128)S(1)}, f32[128,128]{1,0:T(8,128)S(1)}, f32[8,8,64,128]{3,2,1,0:T(8,128)S(1)}) custom-call(s32[2]{0:T(128)S(1)} %pad_add_fusion.refs_0_.place, ...), custom_call_target="tpu_custom_call", output_to_operand_aliasing={{0}: (6, {}), {1}: (7, {})} | custom-call | flops 805306368 | bytes 1048576 | tf_op jit(solution)/shard_map/pallas_call | solution.py:40
  47.2 2.0 %shard_map.25 = (bf16[3,8,512,128]{3,2,1,0:T(8,128)(2,1)S(1)}, f32[8,512,128]{2,1,0:T(8,128)S(1)}, f32[512,256]{1,0:T(8,128)S(1)}, f32[8,8,64,128]{3,2,1,0:T(8,128)S(1)}) custom-call(s32[2]{0:T(128)S(1)} %pad_add_fusion.refs_0_.place, ...), custom_call_target="tpu_custom_call", output_to_operand_aliasing={{0}: (7, {}), {1}: (8, {}), {3}: (9, {})} | custom-call | flops 805306368 | bytes 1048576 | tf_op jit(solution)/shard_map/pallas_call | solution.py:40
  49.2 2.9 %shard_map.26 = f32[8,8,64,128]{3,2,1,0:T(8,128)S(1)} custom-call(s32[2]{0:T(128)S(1)} %pad_add_fusion.refs_0_.place, bf16[8,1,17,16,128]{4,3,2,1,0:T(8,128)(2,1)S(1)} %collective-permute-done.2.right2, bf16[8,1,17,16,128]{4,3,2,1,0:T(8,128)(2,1)S(1)} %collective-permute-done.5.right3, ...), custom_call_target="tpu_custom_call", output_to_operand_aliasing={{}: (6, {})} | custom-call | flops 1073741824 | bytes 1048576 | tf_op jit(solution)/shard_map/pallas_call | solution.py:40
  52.4 28.1 %all_to_all.5 = f16[64,64,128]{2,1,0:T(8,128)(2,1)S(1)} all-to-all(f16[64,64,128]{2,1,0:T(8,128)(2,1)S(1)} %bitcast.3), channel_id=1, replica_groups=mesh['band'=8,'chip'=8,'core'=2] {'chip','band'}, dimensions={0} | all-to-all | bytes 2097152 | tf_op jit(solution)/shard_map/all_to_all | solution.py:327
  80.9 0.6 broadcast_multiply_fusion
  (11 shorter events, 1.0 us)
Async XLA Ops:
  2.1 10.5 %collective-permute-start.6 = (bf16[8,128,128]{2,1,0:T(8,128)(2,1)S(1)}, bf16[8,128,128]{2,1,0:T(8,128)(2,1)S(1)}, u32[]{:S(2)}, u32[]{:S(2)}) collective-permute-start(bf16[8,128,128]{2,1,0:T(8,128)(2,1)S(1)} %get-tuple-element.30), channel_id=1, source_target_pairs={{0,2},{2,4},{4,6},{6,0},{8,10},{10,12},{12,14},{14,8},{1,3},{3,5},... | collective-permute-start | bytes 786440 | tf_op jit(solution)/shard_map/ppermute | solution.py:311
  4.2 8.4 %collective-permute-start.7 = (bf16[8,128,128]{2,1,0:T(8,128)(2,1)S(1)}, bf16[8,128,128]{2,1,0:T(8,128)(2,1)S(1)}, u32[]{:S(2)}, u32[]{:S(2)}) collective-permute-start(bf16[8,128,128]{2,1,0:T(8,128)(2,1)S(1)} %get-tuple-element.31), channel_id=1, source_target_pairs={{0,6},{2,0},{4,2},{6,4},{8,14},{10,8},{12,10},{14,12},{1,7},{3,1},... | collective-permute-start | bytes 786440 | tf_op jit(solution)/shard_map/ppermute | solution.py:311
  6.4 9.3 %collective-permute-start.8 = (bf16[8,128,128]{2,1,0:T(8,128)(2,1)S(1)}, bf16[8,128,128]{2,1,0:T(8,128)(2,1)S(1)}, u32[]{:S(2)}, u32[]{:S(2)}) collective-permute-start(bf16[8,128,128]{2,1,0:T(8,128)(2,1)S(1)} %get-tuple-element.32), channel_id=1, source_target_pairs={{0,8},{2,10},{4,12},{6,14},{8,0},{10,2},{12,4},{14,6},{1,9},{3,11}... | collective-permute-start | bytes 786440 | tf_op jit(solution)/shard_map/ppermute | solution.py:311
  16.7 26.7 %collective-permute-start.9 = (bf16[8,2,17,16,128]{4,3,2,1,0:T(8,128)(2,1)S(1)}, bf16[8,2,17,16,128]{4,3,2,1,0:T(8,128)(2,1)S(1)}, u32[]{:S(2)}, u32[]{:S(2)}) collective-permute-start(bf16[8,2,17,16,128]{4,3,2,1,0:T(8,128)(2,1)S(1)} %shard_map.21.right.own0), channel_id=1, source_target_pairs={{0,1},{1,0},{2,3},{3,2},{4,5},{5,4},{6,7},{7,6},{8,9},{9,8},{10,11... | collective-permute-start | bytes 3342344 | tf_op jit(solution)/shard_map/ppermute | solution.py:314
  16.8 16.6 %collective-permute-start = (bf16[8,128,128]{2,1,0:T(8,128)(2,1)S(1)}, bf16[8,128,128]{2,1,0:T(8,128)(2,1)S(1)}, u32[]{:S(2)}, u32[]{:S(2)}) collective-permute-start(bf16[8,128,128]{2,1,0:T(8,128)(2,1)S(1)} %get-tuple-element.25), channel_id=1, source_target_pairs={{0,4},{2,6},{4,0},{6,2},{8,12},{10,14},{12,8},{14,10},{1,5},{3,7},... | collective-permute-start | bytes 786440 | tf_op jit(solution)/shard_map/ppermute | solution.py:311
  18.3 15.0 %collective-permute-start.1 = (bf16[8,128,128]{2,1,0:T(8,128)(2,1)S(1)}, bf16[8,128,128]{2,1,0:T(8,128)(2,1)S(1)}, u32[]{:S(2)}, u32[]{:S(2)}) collective-permute-start(bf16[8,128,128]{2,1,0:T(8,128)(2,1)S(1)} %get-tuple-element.26), channel_id=1, source_target_pairs={{0,10},{2,12},{4,14},{6,8},{8,2},{10,4},{12,6},{14,0},{1,11},{3,13... | collective-permute-start | bytes 786440 | tf_op jit(solution)/shard_map/ppermute | solution.py:311
  21.8 14.2 %collective-permute-start.3 = (bf16[8,128,128]{2,1,0:T(8,128)(2,1)S(1)}, bf16[8,128,128]{2,1,0:T(8,128)(2,1)S(1)}, u32[]{:S(2)}, u32[]{:S(2)}) collective-permute-start(bf16[8,128,128]{2,1,0:T(8,128)(2,1)S(1)} %get-tuple-element.27), channel_id=1, source_target_pairs={{0,14},{2,8},{4,10},{6,12},{8,6},{10,0},{12,2},{14,4},{1,15},{3,9}... | collective-permute-start | bytes 786440 | tf_op jit(solution)/shard_map/ppermute | solution.py:311
  24.0 16.7 %collective-permute-start.4 = (bf16[8,128,128]{2,1,0:T(8,128)(2,1)S(1)}, bf16[8,128,128]{2,1,0:T(8,128)(2,1)S(1)}, u32[]{:S(2)}, u32[]{:S(2)}) collective-permute-start(bf16[8,128,128]{2,1,0:T(8,128)(2,1)S(1)} %get-tuple-element.28), channel_id=1, source_target_pairs={{0,12},{2,14},{4,8},{6,10},{8,4},{10,6},{12,0},{14,2},{1,13},{3,15... | collective-permute-start | bytes 786440 | tf_op jit(solution)/shard_map/ppermute | solution.py:311
  34.2 15.0 %collective-permute-start.2 = (bf16[8,1,17,16,128]{4,3,2,1,0:T(8,128)(2,1)S(1)}, bf16[8,1,17,16,128]{4,3,2,1,0:T(8,128)(2,1)S(1)}, u32[]{:S(2)}, u32[]{:S(2)}) collective-permute-start(bf16[8,1,17,16,128]{4,3,2,1,0:T(8,128)(2,1)S(1)} %shard_map.18.right2), channel_id=1, source_target_pairs={{0,1},{1,0},{2,3},{3,2},{4,5},{5,4},{6,7},{7,6},{8,9},{9,8},{10,11... | collective-permute-start | bytes 1671176 | tf_op jit(solution)/shard_map/ppermute | solution.py:318
  41.5 7.7 %collective-permute-start.5 = (bf16[8,1,17,16,128]{4,3,2,1,0:T(8,128)(2,1)S(1)}, bf16[8,1,17,16,128]{4,3,2,1,0:T(8,128)(2,1)S(1)}, u32[]{:S(2)}, u32[]{:S(2)}) collective-permute-start(bf16[8,1,17,16,128]{4,3,2,1,0:T(8,128)(2,1)S(1)} %shard_map.19.right3), channel_id=1, source_target_pairs={{0,1},{1,0},{2,3},{3,2},{4,5},{5,4},{6,7},{7,6},{8,9},{9,8},{10,11... | collective-permute-start | bytes 1671176 | tf_op jit(solution)/shard_map/ppermute | solution.py:321
